TPU v7x, 32 devices: a whole 2x2x4 slice. The times are simulated.
32 devices in a mesh: dp: 4 (over y, x), land: 8 (over z, core).
Axes of the slice: x: 2, y: 2, z: 4, core: 2. Of those that a mesh axis runs over, the one named last changes fastest.
Arguments:
- items: bfloat16 [16384, 768], P(('dp', 'land')), may hold values from -1.5 to 1.5
- landmarks: bfloat16 [8192, 768], P('land'), may hold values from -1.5 to 1.5
- scales: float32 [8192], P('land'), may hold values from 0.25 to 1
- eigvecs: bfloat16 [8192, 256], P('land'), may hold values from -0.0625 to 0.0625
- eigvals: float32 [256], replicated, may hold values from 0.5 to 2
Outputs:
- coords: float32 [16384, 256], P(('dp', 'land'))
- gram: float32 [256, 256], replicated
All inputs are finite; a program needn't handle non-finite values.
Results may differ from a plain program's by a relative error of at most 0.0028.
Values may be sent and summed in bfloat16 or wider, within the bound.
No kernel may reach another device: no remote copies, remote signals or barrier semaphores. Data moves between devices by JAX's collectives and lax.ppermute only.
A program may use at most 128 MiB of HBM per device.

v0:
```python
import jax
import jax.numpy as jnp
from jax import lax
from jax.sharding import PartitionSpec as P


def kernel_block(rows, landmarks, scales):
    row_vals = rows.astype(jnp.float32)
    land_vals = landmarks.astype(jnp.float32)
    row_sq = jnp.sum(row_vals * row_vals, axis=1)
    land_sq = jnp.sum(land_vals * land_vals, axis=1)
    cross = jnp.dot(rows, landmarks.T, preferred_element_type=jnp.float32)
    dist = row_sq[:, None] + land_sq[None, :] - 2.0 * cross
    return jnp.exp(-dist * scales[None, :])


def per_device(items, landmarks, scales, eigvecs, eigvals):
    own_rows = items.shape[0]
    rows_all = own_rows * lax.axis_size("dp") * lax.axis_size("land")
    landmark_count = landmarks.shape[0] * lax.axis_size("land")
    kernel = kernel_block(lax.all_gather(items, "land", axis=0, tiled=True), landmarks, scales)
    land_degree = lax.psum(jnp.sum(kernel, axis=0), "dp")
    row_part = jnp.sum(kernel, axis=1)
    scaled = (kernel / jnp.sqrt(land_degree)[None, :]).astype(jnp.bfloat16)
    partial_value = jnp.dot(scaled, eigvecs, preferred_element_type=jnp.float32)
    summed, degrees = (
        lax.psum_scatter(partial_value, "land", scatter_dimension=0, tiled=True),
        lax.psum_scatter(row_part, "land", scatter_dimension=0, tiled=True),
    )
    factor = jnp.sqrt(jnp.float32(rows_all) * jnp.float32(landmark_count))
    coords = summed * (factor / jnp.sqrt(degrees))[:, None] / eigvals[None, :]
    outer = jnp.dot(coords.T, coords, precision=lax.Precision.HIGHEST)
    gram = lax.psum(outer, ("dp", "land")) / jnp.float32(rows_all)
    return (coords, gram)


def solution(mesh):
    return jax.shard_map(
        per_device,
        mesh=mesh,
        in_specs=(P(("dp", "land"), None), P("land", None), P("land"), P("land", None), P()),
        out_specs=(P(("dp", "land"), None), P()),
        check_vma=False,
    )
```

profile of v0, /device:TPU:0, one launch (start us, length us, event | category | flops | bytes accessed | tf_op | source)
XLA Modules:
  0.0 303.2 jit_solution(13520838185477166311)
XLA Ops:
  7.2 0.0 copy-start
  7.2 0.0 all-gather.2.cloned.1.call-start
  7.2 0.7 all-gather.2.cloned.1.call-update
  7.9 0.0 reduce-scatter.2.cloned.1.call-start
  8.0 1.8 multiply_reduce_fusion.1
  9.7 67.3 %all-gather.2.cloned.1.call-done = bf16[4096,768]{1,0:T(8,128)(2,1)} async-done(((bf16[512,768]{1,0:T(8,128)(2,1)}), bf16[4096,768]{1,0:T(8,128)(2,1)}) %all-gather.2.cloned.1.call-update) | async-done | bytes 6291472 | tf_op jit(solution)/shard_map/all_gather | solution.py:21
  77.1 4.1 %multiply_reduce_fusion = f32[4096]{0:T(1024)S(1)} fusion(bf16[4096,768]{1,0:T(8,128)(2,1)} %all-gather.2.cloned.1.call-done), kind=kLoop, calls=%fused_computation.2 | loop fusion | flops 9433088 | bytes 6307840 | tf_op jit(solution)/shard_map/reduce_sum | solution.py:10
  81.2 15.5 %fusion.2 = (f32[4096]{0:T(1024)S(1)}, f32[1024]{0:T(1024)S(1)}, f32[4096,1024]{1,0:T(8,128)}) fusion(f32[1024]{0:T(1024)} %param.7, bf16[4096,768]{1,0:T(8,128)(2,1)} %all-gather.2.cloned.1.call-done, bf16[1024,768]{1,0:T(8,128)(2,1)} %param.6, f32[1024]{0:T(1024)S(1)} %multiply_reduce_fusion.1, f32[4096]{0:T(1024)S(1)} %multiply_reduce_fusion), kind=kOutput, calls=%fused_computation.9 | convolution fusion | flops 6471805952 | bytes 24686592 | tf_op jit(solution)/shard_map/dot_general | solution.py:12
  96.6 9.8 %psum.14 = f32[1024]{0:T(1024)S(1)} all-reduce(f32[1024]{0:T(1024)S(1)} %get-tuple-element.3), channel_id=1, replica_groups=mesh['dp'=4,'land'=8] {'dp'}, use_global_device_ids=true, to_apply=%region_3.0 | all-reduce | flops 1024 | bytes 8192 | tf_op jit(solution)/shard_map/psum | solution.py:22
  106.5 0.0 copy-done
  106.5 0.0 copy-start.3
  106.5 0.0 copy-start.2
  106.5 10.1 %fusion = f32[4096,256]{1,0:T(8,128)} fusion(bf16[1024,256]{1,0:T(8,128)(2,1)S(1)} %copy-done, f32[4096,1024]{1,0:T(8,128)} %get-tuple-element.4, f32[1024]{0:T(1024)S(1)} %sqrt.6), kind=kOutput, calls=%fused_computation.3 | convolution fusion | flops 2155872256 | bytes 21499904 | tf_op jit(solution)/shard_map/dot_general | solution.py:25
  116.5 0.0 reduce-scatter.2.cloned.1.call-update
  116.6 0.0 all-reduce.3.cloned.1.call-start
  116.6 0.0 copy-done.3
  116.6 0.6 dynamic-slice
  117.9 27.3 %all-reduce = f32[4096]{0:T(1024)S(1)} all-reduce(f32[4096]{0:T(1024)S(1)} %get-tuple-element.2), channel_id=3, replica_groups=mesh['dp'=4,'land'=8] {'land'}, use_global_device_ids=true, to_apply=%region_6.0.clone | all-reduce | flops 4096 | bytes 32768
  145.1 0.1 fusion.1
  145.2 18.9 %reduce-scatter.2.cloned.1.call-done = f32[512,256]{1,0:T(8,128)} async-done(((f32[4096,256]{1,0:T(8,128)}), f32[512,256]{1,0:T(8,128)}) %reduce-scatter.2.cloned.1.call-update) | async-done | bytes 524304 | tf_op jit(solution)/shard_map/reduce_scatter | solution.py:27
  164.0 0.0 copy-done.2
  164.0 1.2 multiply_divide_fusion
  165.2 0.0 copy-start.1
  165.2 1.7 fusion.3
  167.0 0.0 all-reduce.3.cloned.1.call-update
  167.0 127.9 %all-reduce.3.cloned.1.call-done = f32[256,256]{1,0:T(8,128)} async-done(((f32[256,256]{1,0:T(8,128)}), f32[256,256]{1,0:T(8,128)}) %all-reduce.3.cloned.1.call-update) | async-done | bytes 262160 | tf_op jit(solution)/shard_map/psum | solution.py:33
  295.0 1.7 broadcast_multiply_fusion
  296.6 0.0 copy-done.1
  (1 shorter events, 0.0 us)
Async XLA Ops:
  7.2 99.3 %copy-start = (bf16[1024,256]{1,0:T(8,128)(2,1)S(1)}, bf16[1024,256]{1,0:T(8,128)(2,1)}, u32[]{:S(2)}) copy-start(bf16[1024,256]{1,0:T(8,128)(2,1)} %param.8) | copy-start | bytes 1572868
  7.2 69.9 %all-gather.2.cloned.1.call-start = ((), (), s32[]{:S(2)}) async-start(), calls=%async_computation.1 | async-start | bytes 7077888 | tf_op jit(solution)/shard_map/all_gather | solution.py:21
  7.9 156.1 %reduce-scatter.2.cloned.1.call-start = ((), (), s32[]{:S(2)}) async-start(), calls=%async_computation.2 | async-start | bytes 4718592 | tf_op jit(solution)/shard_map/reduce_scatter | solution.py:27
  106.5 10.2 %copy-start.3 = (u32[32]{0:T(128)S(1)}, u32[32]{0:T(128)}, u32[]{:S(2)}) copy-start(u32[32]{0:T(128)} %constant.11) | copy-start | bytes 388
  106.5 57.6 %copy-start.2 = (f32[256]{0:T(256)S(1)}, f32[256]{0:T(256)}, u32[]{:S(2)}) copy-start(f32[256]{0:T(256)} %param.9) | copy-start | bytes 3076
  116.6 178.4 %all-reduce.3.cloned.1.call-start = ((), (), s32[]{:S(2)}) async-start(), calls=%async_computation.3 | async-start | bytes 524288 | tf_op jit(solution)/shard_map/psum | solution.py:33
  165.2 131.4 %copy-start.1 = (f32[512,256]{1,0:T(8,128)}, f32[512,256]{1,0:T(8,128)S(1)}, u32[]{:S(2)}) copy-start(f32[512,256]{1,0:T(8,128)S(1)} %multiply_divide_fusion) | copy-start | bytes 1572868
Sparse Core Ops, SparseCore 0:
  9.6 67.4 all-gather.1
  116.7 47.3 reduce-scatter.1
  170.1 124.7 all-reduce.2
where the time goes:
time: 303 us
  waiting for transfers between devices  215 us (71%)
  blocking collectives  37.1 us (12%)
  matrix products  27.3 us (9%)
  between operations  14.5 us (5%)
  other arithmetic  8.79 us (3%)
    psum x1, waiting for transfers between devices, per_device(): gram = lax.psum(outer, ('dp', 'land')) / jnp.float32(rows_all)  128 us
    all_gather x1, waiting for transfers between devices, per_device(): lax.all_gather(items, 'land', axis=0, tiled=True)  67.3 us
    unnamed x1, blocking collectives  27.3 us
    reduce_scatter x1, waiting for transfers between devices, per_device(): lax.psum_scatter(partial_value, 'land', scatter_dimension=0, tiled=True)  18.9 us
    dot_general x1, matrix products, kernel_block(): cross = jnp.dot(rows, landmarks.T, preferred_element_type=jnp.float32)  15.5 us
    dot_general x1, matrix products, per_device(): partial_value = jnp.dot(scaled, eigvecs, preferred_element_type=jnp.float32)  10.1 us
    psum x1, blocking collectives, per_device(): land_degree = lax.psum(jnp.sum(kernel, axis=0), 'dp')  9.82 us
  transfers between devices with their start and end apart: 3, of which 3 were waited for; matrix products, arithmetic and copies ran while one was open for 1% of the time, Pallas kernels for 0%

commit v1 on v0

--- a/solution.py
+++ b/solution.py
@@ -30,7 +30,7 @@
     factor = jnp.sqrt(jnp.float32(rows_all) * jnp.float32(landmark_count))
     coords = summed * (factor / jnp.sqrt(degrees))[:, None] / eigvals[None, :]
     outer = jnp.dot(coords.T, coords, precision=lax.Precision.HIGHEST)
-    gram = lax.psum(outer, ("dp", "land")) / jnp.float32(rows_all)
+    gram = jnp.sum(lax.all_gather(outer, ("dp", "land")), axis=0) / jnp.float32(rows_all)
     return (coords, gram)
 
 

time: 303 us -> 254 us (0.84)
  waiting for transfers between devices: 215 us -> 163 us
    psum x1 -> x0, waiting for transfers between devices: 128 us -> none  [per_device(): gram = lax.psum(outer, ('dp', 'land')) / jnp.float32(rows_all)]
    all_gather x0 -> x1, waiting for transfers between devices: none -> 75.9 us  [per_device(): lax.all_gather(outer, ('dp', 'land'))]
    reduce_sum x0 -> x1, other arithmetic: none -> 3.94 us  [per_device(): jnp.sum(lax.all_gather(outer, ('dp', 'land')), axis=0)]
where the time goes in v1:
time: 254 us
  waiting for transfers between devices  163 us (64%)
  blocking collectives  37.1 us (15%)
  matrix products  27.3 us (11%)
  between operations  14.5 us (6%)
  other arithmetic  11.8 us (5%)
    all_gather x1, waiting for transfers between devices, per_device(): lax.all_gather(outer, ('dp', 'land'))  75.9 us
    all_gather x1, waiting for transfers between devices, per_device(): lax.all_gather(items, 'land', axis=0, tiled=True)  67.3 us
    unnamed x1, blocking collectives  27.3 us
    reduce_scatter x1, waiting for transfers between devices, per_device(): lax.psum_scatter(partial_value, 'land', scatter_dimension=0, tiled=True)  18.9 us
    dot_general x1, matrix products, kernel_block(): cross = jnp.dot(rows, landmarks.T, preferred_element_type=jnp.float32)  15.5 us
    dot_general x1, matrix products, per_device(): partial_value = jnp.dot(scaled, eigvecs, preferred_element_type=jnp.float32)  10.1 us
    psum x1, blocking collectives, per_device(): land_degree = lax.psum(jnp.sum(kernel, axis=0), 'dp')  9.82 us
  transfers between devices with their start and end apart: 3, of which 3 were waited for; matrix products, arithmetic and copies ran while one was open for 1% of the time, Pallas kernels for 0%

profile of v1, /device:TPU:0, one launch (start us, length us, event | category | flops | bytes accessed | tf_op | source)
XLA Modules:
  0.0 254.1 jit_solution(10000682081972979356)
XLA Ops:
  7.2 0.0 copy-start
  7.2 0.0 all-gather.4.cloned.1.call-start
  7.2 0.7 all-gather.4.cloned.1.call-update
  7.9 0.0 reduce-scatter.2.cloned.1.call-start
  8.0 1.8 multiply_reduce_fusion.1
  9.7 67.3 %all-gather.4.cloned.1.call-done = bf16[4096,768]{1,0:T(8,128)(2,1)} async-done(((bf16[512,768]{1,0:T(8,128)(2,1)}), bf16[4096,768]{1,0:T(8,128)(2,1)}) %all-gather.4.cloned.1.call-update) | async-done | bytes 6291472 | tf_op jit(solution)/shard_map/all_gather | solution.py:21
  77.1 4.1 %multiply_reduce_fusion = f32[4096]{0:T(1024)S(1)} fusion(bf16[4096,768]{1,0:T(8,128)(2,1)} %all-gather.4.cloned.1.call-done), kind=kLoop, calls=%fused_computation.2 | loop fusion | flops 9433088 | bytes 6307840 | tf_op jit(solution)/shard_map/reduce_sum | solution.py:10
  81.2 15.5 %fusion.2 = (f32[4096]{0:T(1024)S(1)}, f32[1024]{0:T(1024)S(1)}, f32[4096,1024]{1,0:T(8,128)}) fusion(f32[1024]{0:T(1024)} %param.7, bf16[4096,768]{1,0:T(8,128)(2,1)} %all-gather.4.cloned.1.call-done, bf16[1024,768]{1,0:T(8,128)(2,1)} %param.6, f32[1024]{0:T(1024)S(1)} %multiply_reduce_fusion.1, f32[4096]{0:T(1024)S(1)} %multiply_reduce_fusion), kind=kOutput, calls=%fused_computation.9 | convolution fusion | flops 6471805952 | bytes 24686592 | tf_op jit(solution)/shard_map/dot_general | solution.py:12
  96.6 9.8 %psum.7 = f32[1024]{0:T(1024)S(1)} all-reduce(f32[1024]{0:T(1024)S(1)} %get-tuple-element.3), channel_id=1, replica_groups=mesh['dp'=4,'land'=8] {'dp'}, use_global_device_ids=true, to_apply=%region_3.0 | all-reduce | flops 1024 | bytes 8192 | tf_op jit(solution)/shard_map/psum | solution.py:22
  106.5 0.0 copy-done
  106.5 0.0 copy-start.3
  106.5 0.0 copy-start.2
  106.5 10.1 %fusion = f32[4096,256]{1,0:T(8,128)} fusion(bf16[1024,256]{1,0:T(8,128)(2,1)S(1)} %copy-done, f32[4096,1024]{1,0:T(8,128)} %get-tuple-element.4, f32[1024]{0:T(1024)S(1)} %sqrt.6), kind=kOutput, calls=%fused_computation.3 | convolution fusion | flops 2155872256 | bytes 21499904 | tf_op jit(solution)/shard_map/dot_general | solution.py:25
  116.5 0.0 reduce-scatter.2.cloned.1.call-update
  116.6 0.0 all-gather.6.cloned.1.call-start
  116.6 0.0 copy-done.3
  116.6 0.6 dynamic-slice
  117.9 27.3 %all-reduce = f32[4096]{0:T(1024)S(1)} all-reduce(f32[4096]{0:T(1024)S(1)} %get-tuple-element.2), channel_id=4, replica_groups=mesh['dp'=4,'land'=8] {'land'}, use_global_device_ids=true, to_apply=%region_6.0.clone | all-reduce | flops 4096 | bytes 32768
  145.1 0.1 fusion.1
  145.2 18.9 %reduce-scatter.2.cloned.1.call-done = f32[512,256]{1,0:T(8,128)} async-done(((f32[4096,256]{1,0:T(8,128)}), f32[512,256]{1,0:T(8,128)}) %reduce-scatter.2.cloned.1.call-update) | async-done | bytes 524304 | tf_op jit(solution)/shard_map/reduce_scatter | solution.py:27
  164.0 0.0 copy-done.2
  164.0 1.2 multiply_divide_fusion
  165.2 0.0 copy-start.1
  165.2 1.7 fusion.3
  167.0 0.0 all-gather.6.cloned.1.call-update
  167.0 75.9 %all-gather.6.cloned.1.call-done = f32[8192,256]{1,0:T(8,128)} async-done(((f32[256,256]{1,0:T(8,128)}), f32[8192,256]{1,0:T(8,128)}) %all-gather.6.cloned.1.call-update) | async-done | bytes 8388624 | tf_op jit(solution)/shard_map/all_gather | solution.py:33
  242.9 3.9 %reduce_sum.49 = f32[256,256]{1,0:T(8,128)S(1)} reduce(f32[32,256,256]{2,1,0:T(8,128)} %bitcast.7, f32[]{:T(128)} %constant.1.clone.1), dimensions={0}, to_apply=%region_7.0 | reduce | flops 2031616 | bytes 8650756 | tf_op jit(solution)/shard_map/reduce_sum | solution.py:33
  246.8 0.7 broadcast_multiply_fusion
  247.6 0.0 copy-done.1
  (1 shorter events, 0.0 us)
Async XLA Ops:
  7.2 99.3 %copy-start = (bf16[1024,256]{1,0:T(8,128)(2,1)S(1)}, bf16[1024,256]{1,0:T(8,128)(2,1)}, u32[]{:S(2)}) copy-start(bf16[1024,256]{1,0:T(8,128)(2,1)} %param.8) | copy-start | bytes 1572868
  7.2 69.9 %all-gather.4.cloned.1.call-start = ((), (), s32[]{:S(2)}) async-start(), calls=%async_computation.1 | async-start | bytes 7077888 | tf_op jit(solution)/shard_map/all_gather | solution.py:21
  7.9 156.1 %reduce-scatter.2.cloned.1.call-start = ((), (), s32[]{:S(2)}) async-start(), calls=%async_computation.2 | async-start | bytes 4718592 | tf_op jit(solution)/shard_map/reduce_scatter | solution.py:27
  106.5 10.2 %copy-start.3 = (u32[32]{0:T(128)S(1)}, u32[32]{0:T(128)}, u32[]{:S(2)}) copy-start(u32[32]{0:T(128)} %constant.11) | copy-start | bytes 388
  106.5 57.6 %copy-start.2 = (f32[256]{0:T(256)S(1)}, f32[256]{0:T(256)}, u32[]{:S(2)}) copy-start(f32[256]{0:T(256)} %param.9) | copy-start | bytes 3076
  116.6 126.3 %all-gather.6.cloned.1.call-start = ((), (), s32[]{:S(2)}) async-start(), calls=%async_computation.3 | async-start | bytes 8650752 | tf_op jit(solution)/shard_map/all_gather | solution.py:33
  165.2 82.3 %copy-start.1 = (f32[512,256]{1,0:T(8,128)}, f32[512,256]{1,0:T(8,128)S(1)}, u32[]{:S(2)}) copy-start(f32[512,256]{1,0:T(8,128)S(1)} %multiply_divide_fusion) | copy-start | bytes 1572868
Sparse Core Ops, SparseCore 0:
  9.6 67.4 all-gather.3
  116.7 47.3 reduce-scatter.1
  167.6 75.2 all-gather.5
